TPU v7x, 128 devices: a whole 4x4x4 slice. The times are simulated.
128 devices in a mesh: chan: 4 (over x), rows: 32 (over z, y, core).
Axes of the slice: x: 4, y: 4, z: 4, core: 2. Of those that a mesh axis runs over, the one named last changes fastest.
Arguments:
- residual: float32 [4, 1024, 16384], P('chan', 'rows'), may hold values from -6 to 6
- psf: float32 [4, 2048, 2048], P('chan', 'rows'), may hold values from -2 to 2
- positions: int32 [32, 2], replicated, may hold values from 0 to 15360, as said below
Outputs:
- residual_out: float32 [4, 1024, 16384], P('chan', 'rows')
- normalized: float32 [1024, 16384], P('rows', 'chan')
Inputs may be any that keep to these rules, and one draw needn't show every extreme that they name: positions[k, 0] is a row of the image, 0 to 1023; positions[k, 1] is a column from 1024 to 15360.
All inputs are finite; a program needn't handle non-finite values.
Results may differ from a plain program's by a relative error of at most 0.0001.
Values sent between devices are 32-bit elements; how exact they have to be, the bound alone decides.
No kernel may reach another device: no remote copies, remote signals or barrier semaphores. Data moves between devices by JAX's collectives and lax.ppermute only.
A program may use at most 128 MiB of HBM per device.

v0:
```python
import functools

import jax
import jax.numpy as jnp
from jax import lax
from jax.sharding import Mesh
from jax.sharding import PartitionSpec as P

STEPS = 32
ROWS = ("rows_0", "rows_1", "rows_2")
CHAN_ROWS = ("chan", "rows_0", "rows_1", "rows_2")


def by_axis(shard, axes):
    return functools.reduce(lax.psum, axes, shard)


def on_device(residual, psf, positions):
    chan_id = lax.axis_index("chan")
    nchan = lax.axis_size("chan")
    row_id = lax.axis_index(ROWS)
    nrows = lax.axis_size(ROWS)
    slab = residual.shape[1]
    ncols = residual.shape[2]
    own_psf = psf[0]
    shard_rows = own_psf.shape[0]
    patch = own_psf.shape[1]
    half = patch // 2
    first = row_id * slab
    chan_hot = (jnp.arange(nchan) == chan_id).astype(jnp.float32)
    full_psf = lax.all_gather(own_psf, ROWS, axis=0, tiled=True)
    padded_psf = jnp.pad(full_psf, ((slab, slab), (0, 0)))
    zero = jnp.int32(0)

    def subtract(image, row, col, amount):
        offset = first - row + half
        touches = jnp.logical_and(offset > -slab, offset < patch)
        start = jnp.clip(offset + slab, 0, patch + slab)
        psf_rows = lax.dynamic_slice(padded_psf, (start, zero), (slab, patch))
        window = lax.dynamic_slice(image, (zero, col - half), (slab, patch))
        scale = jnp.where(touches, amount, 0.0)
        return lax.dynamic_update_slice(image, window - scale * psf_rows, (zero, col - half))

    image = residual[0]
    peak_rows = positions[:, 0]
    peak_cols = positions[:, 1]
    inside = jnp.logical_and(peak_rows >= first, peak_rows < first + slab)
    local_rows = jnp.clip(peak_rows - first, 0, slab - 1)
    start_values = jnp.where(inside, image[local_rows, peak_cols], 0.0)
    row_offset = peak_rows[:, None] - peak_rows[None, :] + half - row_id * shard_rows
    col_offset = peak_cols[:, None] - peak_cols[None, :] + half
    owned = (row_offset >= 0) & (row_offset < shard_rows) & (col_offset >= 0) & (col_offset < patch)
    couple = own_psf[jnp.clip(row_offset, 0, shard_rows - 1), jnp.clip(col_offset, 0, patch - 1)]
    couple = jnp.where(owned, couple, 0.0)
    start_table, couple_table = (
        by_axis(chan_hot[:, None] * start_values[None, :], CHAN_ROWS),
        by_axis(chan_hot[:, None, None] * couple[None, :, :], CHAN_ROWS),
    )

    def solve(k, amps):
        taken = jnp.sum(amps * lax.dynamic_index_in_dim(couple_table, k, 1, False), axis=1)
        value = lax.dynamic_index_in_dim(start_table, k, 1, False) - taken
        amp = 0.25 * (value + jnp.sum(value) / nchan)
        return lax.dynamic_update_index_in_dim(amps, amp, k, 1)

    amps = lax.fori_loop(0, STEPS, solve, jnp.zeros((nchan, STEPS), jnp.float32))
    own_amps = jnp.sum(chan_hot[:, None] * amps, axis=0)

    def apply(k, image):
        return subtract(image, positions[k, 0], positions[k, 1], own_amps[k])

    image = lax.fori_loop(0, STEPS, apply, image)
    count = slab * nrows * ncols
    parts = lax.psum_scatter(image, "chan", scatter_dimension=1, tiled=True)
    total = by_axis(jnp.sum(parts * parts), CHAN_ROWS)
    normalized = parts * lax.rsqrt(total / count + 1e-06)
    return (image[None], normalized)


def solution(mesh):
    finer = Mesh(
        mesh.devices.reshape(mesh.shape["chan"], 4, 4, 2), ("chan", "rows_0", "rows_1", "rows_2")
    )
    return jax.shard_map(
        on_device,
        mesh=finer,
        in_specs=(P("chan", ROWS, None), P("chan", ROWS, None), P()),
        out_specs=(P("chan", ROWS, None), P(ROWS, "chan")),
        check_vma=False,
    )
```

profile of v0, /device:TPU:1, one launch (start us, length us, event | category | flops | bytes accessed | tf_op | source)
XLA Modules:
  0.0 407.3 jit_solution(14780614954989657997)
XLA Ops:
  7.2 1.6 copy.28
  9.2 8.6 %gather_fusion.1 = f32[1024]{0:T(1024)S(1)} fusion(f32[64,2048]{1,0:T(8,128)S(1)} %bitcast.46, s32[1024]{0:T(1024)S(1)} %reshape.252), kind=kCustom, calls=%fused_computation.1 | custom fusion | bytes 16384 | tf_op jit(solution)/shard_map/gather | solution.py:53
  18.8 16.1 %all-reduce.3 = (f32[4,32]{1,0:T(4,128)S(1)}, f32[4,32,32]{2,0,1:T(4,128)S(1)}) all-reduce(f32[4,32]{1,0:T(4,128)S(1)} %broadcast_multiply_fusion.2, f32[4,32,32]{2,0,1:T(4,128)S(1)} %broadcast_multiply_fusion.1), channel_id=1, replica_groups=mesh['chan'=4,'rows_0'=4,'rows_1'=4,'rows_2'=2] {'chan'}, use_global_device_ids=true, to_apply=%region_4.5 | all-reduce | flops 4224 | bytes 33792 | tf_op jit(solution)/shard_map/psum | solution.py:15
  34.9 15.7 %all-reduce.2 = (f32[4,32]{1,0:T(4,128)S(1)}, f32[4,32,32]{2,0,1:T(4,128)S(1)}) all-reduce(f32[4,32]{1,0:T(4,128)S(1)} %get-tuple-element.307, f32[4,32,32]{2,0,1:T(4,128)S(1)} %get-tuple-element.308), channel_id=1, replica_groups=mesh['chan'=4,'rows_0'=4,'rows_1'=4,'rows_2'=2] {'rows_0'}, use_global_device_ids=true, to_apply=%region_5.6 | all-reduce | flops 4224 | bytes 33792 | tf_op jit(solution)/shard_map/psum | solution.py:15
  50.6 18.6 %all-reduce.1 = (f32[4,32]{1,0:T(4,128)S(1)}, f32[4,32,32]{2,0,1:T(4,128)S(1)}) all-reduce(f32[4,32]{1,0:T(4,128)S(1)} %get-tuple-element.305, f32[4,32,32]{2,0,1:T(4,128)S(1)} %get-tuple-element.306), channel_id=1, replica_groups=mesh['chan'=4,'rows_0'=4,'rows_1'=4,'rows_2'=2] {'rows_1'}, use_global_device_ids=true, to_apply=%region_6.7 | all-reduce | flops 4224 | bytes 33792 | tf_op jit(solution)/shard_map/psum | solution.py:15
  69.2 12.4 %all-reduce.4 = (f32[4,32]{1,0:T(4,128)S(1)}, f32[4,32,32]{2,0,1:T(4,128)S(1)}) all-reduce(f32[4,32]{1,0:T(4,128)S(1)} %get-tuple-element.303, f32[4,32,32]{2,0,1:T(4,128)S(1)} %get-tuple-element.304), channel_id=1, replica_groups=mesh['chan'=4,'rows_0'=4,'rows_1'=4,'rows_2'=2] {'rows_2'}, use_global_device_ids=true, to_apply=%region_7.8 | all-reduce | flops 4224 | bytes 33792 | tf_op jit(solution)/shard_map/psum | solution.py:15
  81.6 57.8 %while.30 = (s32[]{:T(128)}, f32[4,32]{1,0:T(4,128)S(1)}, f32[4,32]{1,0:T(4,128)S(1)}, f32[4,32,32]{2,0,1:T(4,128)S(1)}, s32[]{:T(128)}, /*index=5*/f32[]{:T(128)}, s32[]{:T(128)}) while((s32[]{:T(128)}, f32[4,32]{1,0:T(4,128)S(1)}, f32[4,32]{1,0:T(4,128)S(1)}, f32[4,32,32]{2,0,1:T(4,128)S(1)}, s32[]{:T(128)}, /*index=5*/f32[]{:T(128)}, ...), condition=%wide.region_11.12_spmd, body=%wide.region_8.11_spmd.sunk | while | flops 274 | bytes 2329 | solution.py:66
  139.5 11.7 %pad.4 = f32[2112,2048]{1,0:T(8,128)} pad(f32[2048,2048]{1,0:T(8,128)} %bitcast.50, f32[]{:T(128)} %constant.215.clone.1), padding=32_32x0_0 | pad | bytes 34078724 | tf_op jit(solution)/shard_map/jit(_pad)/pad | solution.py:32
  151.3 183.0 %while.31 = (s32[]{:T(128)}, f32[32,16384]{1,0:T(8,128)S(1)}, s32[32,2]{0,1:T(2,128)S(1)}, s32[]{:T(128)}, f32[32]{0:T(128)S(1)}, /*index=5*/f32[2112,2048]{1,0:...) while((s32[]{:T(128)}, f32[32,16384]{1,0:T(8,128)S(1)}, ...), condition=%wide.region_14.15_spmd, body=%wide.region_13.14_spmd.sunk | while | flops 131087 | bytes 1311065 | solution.py:72
  155.1 1.1 multiply_subtract_fusion.2
  160.8 1.1 multiply_subtract_fusion.2
  166.5 1.1 multiply_subtract_fusion.2
  172.2 1.1 multiply_subtract_fusion.2
  177.9 1.1 multiply_subtract_fusion.2
  183.6 1.1 multiply_subtract_fusion.2
  189.3 1.1 multiply_subtract_fusion.2
  195.0 1.1 multiply_subtract_fusion.2
  200.7 1.1 multiply_subtract_fusion.2
  206.4 1.1 multiply_subtract_fusion.2
  212.1 1.1 multiply_subtract_fusion.2
  217.8 1.1 multiply_subtract_fusion.2
  223.5 1.1 multiply_subtract_fusion.2
  229.2 1.1 multiply_subtract_fusion.2
  234.9 1.1 multiply_subtract_fusion.2
  240.6 1.1 multiply_subtract_fusion.2
  246.3 1.1 multiply_subtract_fusion.2
  252.2 1.1 multiply_subtract_fusion.2
  257.9 1.1 multiply_subtract_fusion.2
  263.9 1.1 multiply_subtract_fusion.2
  269.6 1.1 multiply_subtract_fusion.2
  275.3 1.1 multiply_subtract_fusion.2
  281.0 1.1 multiply_subtract_fusion.2
  286.4 1.1 multiply_subtract_fusion.2
  292.1 1.1 multiply_subtract_fusion.2
  297.8 1.1 multiply_subtract_fusion.2
  303.5 1.1 multiply_subtract_fusion.2
  309.2 1.1 multiply_subtract_fusion.2
  320.6 1.1 multiply_subtract_fusion.2
  326.3 1.1 multiply_subtract_fusion.2
  332.4 1.1 multiply_subtract_fusion.2
  334.2 1.3 copy-done.1
  335.6 25.5 %reduce-scatter.2.cloned.1.call-done = f32[32,4096]{1,0:T(8,128)} async-done(((f32[32,16384]{1,0:T(8,128)}), f32[32,4096]{1,0:T(8,128)}) %reduce-scatter.2.cloned.1.call-update) | async-done | bytes 524304 | tf_op jit(solution)/shard_map/reduce_scatter | solution.py:74
  361.1 1.8 multiply_reduce_fusion
  362.9 7.2 %psum.92 = f32[]{:T(128)} all-reduce(f32[]{:T(128)} %multiply_reduce_fusion), channel_id=1, replica_groups=mesh['chan'=4,'rows_0'=4,'rows_1'=4,'rows_2'=2] {'chan'}, use_global_device_ids=true, to_apply=%region_17.18 | all-reduce | flops 1 | bytes 8 | tf_op jit(solution)/shard_map/psum | solution.py:15
  370.1 9.6 %psum.93 = f32[]{:T(128)} all-reduce(f32[]{:T(128)} %psum.92), channel_id=1, replica_groups=mesh['chan'=4,'rows_0'=4,'rows_1'=4,'rows_2'=2] {'rows_0'}, use_global_device_ids=true, to_apply=%region_18.19 | all-reduce | flops 1 | bytes 8 | tf_op jit(solution)/shard_map/psum | solution.py:15
  379.6 8.7 %psum.94 = f32[]{:T(128)} all-reduce(f32[]{:T(128)} %psum.93), channel_id=1, replica_groups=mesh['chan'=4,'rows_0'=4,'rows_1'=4,'rows_2'=2] {'rows_1'}, use_global_device_ids=true, to_apply=%region_19.20 | all-reduce | flops 1 | bytes 8 | tf_op jit(solution)/shard_map/psum | solution.py:15
  388.4 9.5 %psum.95 = f32[]{:T(128)} all-reduce(f32[]{:T(128)} %psum.94), channel_id=1, replica_groups=mesh['chan'=4,'rows_0'=4,'rows_1'=4,'rows_2'=2] {'rows_2'}, use_global_device_ids=true, to_apply=%region_20.21 | all-reduce | flops 1 | bytes 8 | tf_op jit(solution)/shard_map/psum | solution.py:15
  398.6 1.9 broadcast_multiply_fusion
  (311 shorter events, 99.1 us)
Async XLA Ops:
  7.2 2.0 copy-start
  7.2 1.8 copy-start.2
  7.2 132.3 %all-gather.3.cloned.1.call-start = ((), (), s32[]{:S(2)}) async-start(), calls=%async_computation.2 | async-start | bytes 17301504 | tf_op jit(solution)/shard_map/all_gather | solution.py:31
  8.9 352.2 %reduce-scatter.2.cloned.1.call-start = ((), (), s32[]{:S(2)}) async-start(), calls=%async_computation.1 | async-start | bytes 2621440 | tf_op jit(solution)/shard_map/reduce_scatter | solution.py:74
  334.2 1.3 copy-start.1
Sparse Core Ops, SparseCore 0:
  10.3 77.2 all-gather.2
  335.7 25.3 reduce-scatter.1
where the time goes:
time: 411 us; the launch traced here: 407 us
  loops' own time  108 us (26%)
  blocking collectives  97.8 us (24%)
  local copies, waits for them, and re-layouts  94.3 us (23%)
  other arithmetic  66.3 us (16%)
  waiting for transfers between devices  25.6 us (6%)
  between operations  14.9 us (4%)
    psum x8, blocking collectives, by_axis(): return functools.reduce(lax.psum, axes, shard)  97.8 us
    another operation x1, loops' own time, on_device(): image = lax.fori_loop(0, STEPS, apply, image)  85.9 us
    dynamic_slice x64, local copies, waits for them, and re-layouts, apply(): return subtract(image, positions[k, 0], positions[k, 1], own_amps[k])  39.9 us
    sub x32, other arithmetic, subtract(): window - scale * psf_rows  35.8 us
    reduce_scatter x1, waiting for transfers between devices, on_device(): parts = lax.psum_scatter(image, 'chan', scatter_dimension=1, tiled=True)  25.5 us
    another operation x1, loops' own time, on_device(): lax.fori_loop(0, STEPS, solve, jnp.zeros((nchan, STEPS), jnp.float32))  22.5 us
    reduce_sum x32, other arithmetic, solve(): amp = 0.25 * (value + jnp.sum(value) / nchan)  22.1 us
    dynamic_update_slice x32, local copies, waits for them, and re-layouts, subtract(): lax.dynamic_update_slice(image, window - scale * psf_rows, (zero, col - h...  21.4 us
  transfers between devices with their start and end apart: 2, of which 1 were waited for; matrix products, arithmetic and copies ran while one was open for 11% of the time, Pallas kernels for 0%

commit v1 on v0

v1 whole, which is shorter than its diff:
```python
import functools

import jax
import jax.numpy as jnp
from jax import lax
from jax.experimental import pallas as pl
from jax.experimental.pallas import tpu as pltpu
from jax.sharding import Mesh
from jax.sharding import PartitionSpec as P

STEPS = 32
ROWS = ("rows_0", "rows_1", "rows_2")
CHAN_ROWS = ("chan", "rows_0", "rows_1", "rows_2")
LANES = 128
SUBLANES = 8
DEVICES = 128
NCHAN = 4
SLAB = 32
SHARD = 64
PATCH = 2048
HALF = PATCH // 2
NCOL = 16384
TALL = SLAB + SUBLANES
FOLD = LANES // STEPS


def floor_to(x, size):
    return pl.multiple_of(x - (x & (size - 1)), size)


def table_kernel(pos_ref, id_ref, psf_ref, res_ref, out_ref, tiles, wide, acc, sems):
    row_id = id_ref[0]
    first = row_id * SLAB
    lane = lax.broadcasted_iota(jnp.int32, (SUBLANES, LANES), 1)
    cell = lax.broadcasted_iota(jnp.int32, (SUBLANES, LANES), 0) * LANES + lane

    def tile_copy(k):
        local = jnp.clip(pos_ref[2 * k] - first, 0, SLAB - 1)
        src = res_ref.at[pl.ds(floor_to(local, SUBLANES), SUBLANES), pl.ds(floor_to(pos_ref[2 * k + 1], LANES), LANES)]
        return pltpu.make_async_copy(src, tiles.at[k], sems.at[k])

    def placed(tile, row, col, target, owned):
        turned = pltpu.roll(tile, (target - col) & (LANES - 1), 1)
        return cell == jnp.where(owned, (row & (SUBLANES - 1)) * LANES + target, -1), turned

    for k in range(STEPS):
        tile_copy(k).start()
    sums = [jnp.zeros((SUBLANES, LANES), jnp.float32) for _ in range(STEPS // FOLD)]
    for k in range(STEPS):
        base_row = pos_ref[2 * k] + HALF - row_id * SHARD
        base_col = pos_ref[2 * k + 1] + HALF
        for l in range(k):
            row = base_row - pos_ref[2 * l]
            col = base_col - pos_ref[2 * l + 1]
            owned = (row >= 0) & (row < SHARD) & (col >= 0) & (col < PATCH)
            row = jnp.clip(row, 0, SHARD - 1)
            col = jnp.clip(col, 0, PATCH - 1)
            tile = psf_ref[pl.ds(floor_to(row, SUBLANES), SUBLANES), pl.ds(floor_to(col, LANES), LANES)]
            here, turned = placed(tile, row, col, STEPS * (k % FOLD) + l, owned)
            sums[k // FOLD] = jnp.where(here, turned, sums[k // FOLD])
        if k % FOLD == FOLD - 1:
            wide[k // FOLD] = sums[k // FOLD]
    for k in range(STEPS):
        tile_copy(k).wait()
        local = pos_ref[2 * k] - first
        owned = (local >= 0) & (local < SLAB)
        here, turned = placed(tiles[k], jnp.clip(local, 0, SLAB - 1), pos_ref[2 * k + 1], STEPS * (k % FOLD) + k, owned)
        wide[k // FOLD] = jnp.where(here, turned, wide[k // FOLD])
    for g in range(STEPS // FOLD):
        acc[g : g + 1, :] = jnp.sum(wide[g], axis=0, keepdims=True)
    out_ref[...] = jnp.broadcast_to(acc[...][None], (DEVICES, SUBLANES, LANES))


def table(pos, ids, psf, residual):
    return pl.pallas_call(
        table_kernel,
        out_shape=jax.ShapeDtypeStruct((DEVICES, SUBLANES, LANES), jnp.float32),
        in_specs=[
            pl.BlockSpec(memory_space=pltpu.SMEM),
            pl.BlockSpec(memory_space=pltpu.SMEM),
            pl.BlockSpec(memory_space=pltpu.VMEM),
            pl.BlockSpec(memory_space=pl.ANY),
        ],
        out_specs=pl.BlockSpec(memory_space=pltpu.VMEM),
        scratch_shapes=[
            pltpu.VMEM((STEPS, SUBLANES, LANES), jnp.float32),
            pltpu.VMEM((SUBLANES, SUBLANES, LANES), jnp.float32),
            pltpu.VMEM((SUBLANES, LANES), jnp.float32),
            pltpu.SemaphoreType.DMA((STEPS,)),
        ],
        name="table",
    )(pos, ids, psf, residual)


def solve_kernel(id_ref, parts_ref, out_ref, rows):
    chan_id = id_ref[1]
    per_chan = DEVICES // NCHAN
    for c in range(NCHAN):
        summed = parts_ref[c * per_chan]
        for d in range(1, per_chan):
            summed = summed + parts_ref[c * per_chan + d]
        for g in range(SUBLANES):
            rows[g, c : c + 1, :] = summed[g : g + 1, :]
            rows[g, NCHAN + c : NCHAN + c + 1, :] = jnp.zeros((1, LANES), jnp.float32)
    lane = lax.broadcasted_iota(jnp.int32, (SUBLANES, LANES), 1)
    sub = lax.broadcasted_iota(jnp.int32, (SUBLANES, LANES), 0)
    at = lane % STEPS
    group = lane // STEPS
    own = sub == chan_id
    amps = jnp.zeros((SUBLANES, LANES), jnp.float32)
    for k in range(STEPS):
        weights = jnp.where(at == k, -1.0, amps)
        products = jnp.where(group == k % FOLD, rows[k // FOLD] * weights, 0.0)
        value = -jnp.sum(products, axis=1, keepdims=True)
        total = jnp.sum(value, axis=0, keepdims=True)
        amp = jnp.broadcast_to(0.25 * (value + total / NCHAN), (SUBLANES, LANES))
        amps = jnp.where((at == k) & (sub < NCHAN), amp, amps)
        mine = jnp.sum(jnp.where(own, amp, 0.0), axis=0, keepdims=True)
        out_ref[k] = jnp.broadcast_to(mine, (SUBLANES, LANES))


def solve(ids, parts):
    return pl.pallas_call(
        solve_kernel,
        out_shape=jax.ShapeDtypeStruct((STEPS, SUBLANES, LANES), jnp.float32),
        in_specs=[pl.BlockSpec(memory_space=pltpu.SMEM), pl.BlockSpec(memory_space=pltpu.VMEM)],
        out_specs=pl.BlockSpec(memory_space=pltpu.VMEM),
        scratch_shapes=[pltpu.VMEM((SUBLANES, SUBLANES, LANES), jnp.float32)],
        name="solve",
    )(ids, parts)


def apply_kernel(pos_ref, id_ref, amps_ref, psf_ref, res_ref, out_ref, image, windows, sems, edge_sems):
    first = id_ref[0] * SLAB
    lane = lax.broadcasted_iota(jnp.int32, (SUBLANES, LANES), 1)
    sub = lax.broadcasted_iota(jnp.int32, (SUBLANES, LANES), 0)

    def start_row(k):
        start = first - pos_ref[2 * k] + HALF
        return start, pl.multiple_of(jnp.minimum(start - (start & (SUBLANES - 1)), PATCH - TALL), SUBLANES)

    def window_copy(k):
        return pltpu.make_async_copy(psf_ref.at[pl.ds(start_row(k)[1], TALL), :], windows.at[k], sems.at[k])

    load = pltpu.make_async_copy(res_ref, image.at[:, pl.ds(0, NCOL)], edge_sems.at[0])
    load.start()
    lax.fori_loop(0, STEPS, lambda k, _: (window_copy(k).start(), 0)[1], 0)
    load.wait()

    def peak(k, _):
        window_copy(k).wait()
        start, aligned = start_row(k)
        off = start - aligned
        left = pos_ref[2 * k + 1] - HALF
        shift = left & (LANES - 1)
        base = left - shift
        amp = amps_ref[k]
        carried = lane < shift
        upper = sub < SUBLANES - off
        groups = TALL // SUBLANES
        before = [jnp.zeros((SUBLANES, LANES), jnp.float32)] * groups
        for t in range(PATCH // LANES + 1):
            if t < PATCH // LANES:
                turned = [
                    pltpu.roll(windows[k, pl.ds(g * SUBLANES, SUBLANES), pl.ds(t * LANES, LANES)], shift, 1)
                    for g in range(groups)
                ]
            else:
                turned = [jnp.zeros((SUBLANES, LANES), jnp.float32)] * groups
            joined = [pltpu.roll(jnp.where(carried, b, n), (SUBLANES - off) & (SUBLANES - 1), 0) for b, n in zip(before, turned)]
            cols = pl.ds(pl.multiple_of(base + t * LANES, LANES), LANES)
            for g in range(SLAB // SUBLANES):
                rows = pl.ds(g * SUBLANES, SUBLANES)
                image[rows, cols] = image[rows, cols] - amp * jnp.where(upper, joined[g], joined[g + 1])
            before = turned
        return 0

    lax.fori_loop(0, STEPS, peak, 0)
    store = pltpu.make_async_copy(image.at[:, pl.ds(0, NCOL)], out_ref, edge_sems.at[1])
    store.start()
    store.wait()


def apply(pos, ids, amps, psf, residual):
    return pl.pallas_call(
        apply_kernel,
        out_shape=jax.ShapeDtypeStruct((SLAB, NCOL), jnp.float32),
        in_specs=[
            pl.BlockSpec(memory_space=pltpu.SMEM),
            pl.BlockSpec(memory_space=pltpu.SMEM),
            pl.BlockSpec(memory_space=pltpu.VMEM),
            pl.BlockSpec(memory_space=pl.ANY),
            pl.BlockSpec(memory_space=pl.ANY),
        ],
        out_specs=pl.BlockSpec(memory_space=pl.ANY),
        scratch_shapes=[
            pltpu.VMEM((SLAB, NCOL + LANES), jnp.float32),
            pltpu.VMEM((STEPS, TALL, PATCH), jnp.float32),
            pltpu.SemaphoreType.DMA((STEPS,)),
            pltpu.SemaphoreType.DMA((2,)),
        ],
        compiler_params=pltpu.CompilerParams(vmem_limit_bytes=32 << 20),
        name="apply",
    )(pos, ids, amps, psf, residual)


def on_device(residual, psf, positions):
    chan_id = lax.axis_index("chan")
    row_id = lax.axis_index(ROWS)
    nrows = lax.axis_size(ROWS)
    slab, ncols = residual.shape[1:]
    ids = jnp.stack([row_id, chan_id]).astype(jnp.int32)
    pos = positions.reshape(-1)
    full_psf = lax.all_gather(psf[0], ROWS, axis=0, tiled=True)
    parts = table(pos, ids, psf[0], residual[0])
    parts = lax.all_to_all(parts, CHAN_ROWS, 0, 0, tiled=True)
    amps = solve(ids, parts)
    image = apply(pos, ids, amps, full_psf, residual[0])
    summed = lax.psum_scatter(image, "chan", scatter_dimension=1, tiled=True)
    square = jnp.broadcast_to(jnp.sum(summed * summed), (DEVICES, 1, LANES))
    total = jnp.sum(lax.all_to_all(square, CHAN_ROWS, 0, 0, tiled=True)[:, 0, 0])
    count = slab * nrows * ncols
    normalized = summed * lax.rsqrt(total / count + 1e-06)
    return (image[None], normalized)


def solution(mesh):
    finer = Mesh(
        mesh.devices.reshape(mesh.shape["chan"], 4, 4, 2), ("chan", "rows_0", "rows_1", "rows_2")
    )
    return jax.shard_map(
        on_device,
        mesh=finer,
        in_specs=(P("chan", ROWS, None), P("chan", ROWS, None), P()),
        out_specs=(P("chan", ROWS, None), P(ROWS, "chan")),
        check_vma=False,
    )
```

time: 411 us -> 169 us (0.41)
  loops' own time: 108 us -> 0 us
  local copies, waits for them, and re-layouts: 94.3 us -> 8.74 us
  other arithmetic: 66.3 us -> 5.03 us
  blocking collectives: 97.8 us -> 42.5 us
  waiting for transfers between devices: 25.6 us -> 70 us
  Pallas kernels: 0 us -> 27.2 us
    another operation x2 -> x0, loops' own time: 108 us -> none  [the longest x1 85.9 us: on_device(): image = lax.fori_loop(0, STEPS, apply, image)]
    psum x8 -> x0, blocking collectives: 97.8 us -> none  [by_axis(): return functools.reduce(lax.psum, axes, shard)]
    all_to_all x0 -> x2, blocking collectives: none -> 42.5 us  [the longest x1 25.1 us: on_device(): parts = lax.all_to_all(parts, CHAN_ROWS, 0, 0, tiled=True)]
    all_gather x1, waiting for transfers between devices: 0.01 us -> 40.6 us  [on_device(): full_psf = lax.all_gather(psf[0], ROWS, axis=0, tiled=True)]
    dynamic_slice x64 -> x0, local copies, waits for them, and re-layouts: 39.9 us -> none  [apply(): return subtract(image, positions[k, 0], positions[k, 1], own_amps[k])]
    sub x33 -> x0, other arithmetic: 35.8 us -> none  [the longest x32 35.8 us: subtract(): window - scale * psf_rows]
    pallas_call x0 -> x3, Pallas kernels: none -> 27.2 us  [the longest x1 11.4 us: apply(): pl.pallas_call(apply_kernel, out_shape=jax.ShapeDtypeStruct((SLAB, NCOL),...]
    reduce_sum x66 -> x2, other arithmetic: 27.8 us -> 2.51 us  [the longest x1 1.78 us: on_device(): square = jnp.broadcast_to(jnp.sum(summed * summed), (DEVICES, 1, LANES))]
  transfers between devices with their start and end apart: 2 -> 2, of which waited for: 1 -> 2; matrix products, arithmetic and copies ran while one was open for 11% -> 1% of each run, Pallas kernels for 0% -> 9%
where the time goes in v1:
time: 169 us; the launch traced here: 168 us
  waiting for transfers between devices  70 us (41%)
  blocking collectives  42.5 us (25%)
  Pallas kernels  27.2 us (16%)
  between operations  14.8 us (9%)
  local copies, waits for them, and re-layouts  8.74 us (5%)
  other arithmetic  5.03 us (3%)
    all_gather x1, waiting for transfers between devices, on_device(): full_psf = lax.all_gather(psf[0], ROWS, axis=0, tiled=True)  40.6 us
    reduce_scatter x1, waiting for transfers between devices, on_device(): summed = lax.psum_scatter(image, 'chan', scatter_dimension=1, tiled=True)  28.8 us
    all_to_all x1, blocking collectives, on_device(): parts = lax.all_to_all(parts, CHAN_ROWS, 0, 0, tiled=True)  25.1 us
    all_to_all x1, blocking collectives, on_device(): lax.all_to_all(square, CHAN_ROWS, 0, 0, tiled=True)[:, 0, 0]  17.4 us
    pallas_call x1, Pallas kernels, apply(): pl.pallas_call(apply_kernel, out_shape=jax.ShapeDtypeStruct((SLAB, NCOL),...  11.4 us
    pallas_call x1, Pallas kernels, table(): pl.pallas_call(table_kernel, out_shape=jax.ShapeDtypeStruct((DEVICES, SUB...  11.2 us
    unnamed x11, local copies, waits for them, and re-layouts  7.44 us
    pallas_call x1, Pallas kernels, solve(): pl.pallas_call(solve_kernel, out_shape=jax.ShapeDtypeStruct((STEPS, SUBLA...  4.59 us
  transfers between devices with their start and end apart: 2, of which 2 were waited for; matrix products, arithmetic and copies ran while one was open for 1% of the time, Pallas kernels for 9%

profile of v1, /device:TPU:1, one launch (start us, length us, event | category | flops | bytes accessed | tf_op | source)
XLA Modules:
  0.0 168.4 jit_solution(2238509115078930600)
XLA Ops:
  7.2 0.0 all-gather.3.cloned.1.call-start
  7.2 0.7 all-gather.3.cloned.1.call-update
  7.9 0.0 reduce-scatter.2.cloned.1.call-start
  8.0 0.8 copy.8
  8.7 0.6 reshape.7.pos_ref
  9.3 0.6 pad_add_fusion.id_ref
  10.0 0.0 copy-start.1
  10.0 0.0 copy-start.3
  10.0 0.0 copy-start.4
  10.0 11.2 %table.1 = f32[128,8,128]{2,1,0:T(8,128)} custom-call(s32[64]{0:T(128)} %reshape.7.pos_ref, s32[2]{0:T(128)} %pad_add_fusion.id_ref, f32[64,2048]{1,0:T(8,128)} %bitcast.10, f32[32,16384]{1,0:T(8,128)} %bitcast.7), custom_call_target="tpu_custom_call" | custom-call | tf_op jit(solution)/shard_map/table/pallas_call | solution.py:75
  21.2 25.1 %all_to_all.10.parts_ref = f32[128,8,128]{2,1,0:T(8,128)} all-to-all(f32[128,8,128]{2,1,0:T(8,128)} %table.1), channel_id=1, replica_groups=mesh['chan'=4,'rows_0'=4,'rows_1'=4,'rows_2'=2] {'chan','rows_0','rows_1..., dimensions={0} | all-to-all | bytes 1048576 | tf_op jit(solution)/shard_map/all_to_all | solution.py:216
  46.3 4.6 %solve.1.amps_ref = f32[32,8,128]{2,1,0:T(8,128)} custom-call(s32[2]{0:T(128)} %pad_add_fusion.id_ref, f32[128,8,128]{2,1,0:T(8,128)} %all_to_all.10.parts_ref), custom_call_target="tpu_custom_call" | custom-call | tf_op jit(solution)/shard_map/solve/pallas_call | solution.py:123
  50.9 40.6 %all-gather.3.cloned.1.call-done = f32[1,2048,2048]{2,1,0:T(8,128)} async-done(((f32[1,64,2048]{2,1,0:T(8,128)}), f32[1,2048,2048]{2,1,0:T(8,128)}) %all-gather.3.cloned.1.call-update) | async-done | bytes 16777232 | tf_op jit(solution)/shard_map/all_gather | solution.py:214
  91.5 0.0 copy-done.1
  91.5 0.0 copy-done.3
  91.5 0.0 copy-done.4
  91.5 0.0 copy-start
  91.5 5.8 %copy-done = f32[1,2048,2048]{2,1,0:T(8,128)S(1)} copy-done((f32[1,2048,2048]{2,1,0:T(8,128)S(1)}, f32[1,2048,2048]{2,1,0:T(8,128)}, u32[]{:S(2)}) %copy-start) | copy-done | bytes 16777240
  97.3 0.0 copy-start.2
  97.3 0.9 copy-done.2
  98.2 11.4 %apply.1 = f32[32,16384]{1,0:T(8,128)} custom-call(s32[64]{0:T(128)S(1)} %copy-done.3, s32[2]{0:T(128)S(1)} %copy-done.4, f32[32,8,128]{2,1,0:T(8,128)S(1)} %copy-done.2, f32[2048,2048]{1,0:T(8,128)S(1)} %bitcast.6, f32[32,16384]{1,0:T(8,128)S(1)} %bitcast.8), custom_call_target="tpu_custom_call" | custom-call | tf_op jit(solution)/shard_map/apply/pallas_call | solution.py:185
  109.6 0.0 reduce-scatter.2.cloned.1.call-update
  109.6 28.8 %reduce-scatter.2.cloned.1.call-done = f32[32,4096]{1,0:T(8,128)} async-done(((f32[32,16384]{1,0:T(8,128)}), f32[32,4096]{1,0:T(8,128)}) %reduce-scatter.2.cloned.1.call-update) | async-done | bytes 524304 | tf_op jit(solution)/shard_map/reduce_scatter | solution.py:219
  138.4 1.8 %multiply_reduce_fusion = f32[]{:T(128)} fusion(f32[32,4096]{1,0:T(8,128)} %reduce-scatter.2.cloned.1.call-done), kind=kLoop, calls=%fused_computation | loop fusion | flops 262143 | bytes 524292 | tf_op jit(solution)/shard_map/reduce_sum | solution.py:220
  140.1 0.7 broadcast_in_dim.7
  140.8 17.4 %all_to_all.11 = f32[128,1,128]{2,1,0:T(1,128)S(1)} all-to-all(f32[128,1,128]{2,1,0:T(1,128)S(1)} %broadcast_in_dim.7), channel_id=1, replica_groups=mesh['chan'=4,'rows_0'=4,'rows_1'=4,'rows_2'=2] {'chan','rows_0','rows_1..., dimensions={0} | all-to-all | bytes 131072 | tf_op jit(solution)/shard_map/all_to_all | solution.py:221
  158.2 0.7 slice_reduce_fusion
  159.7 1.9 %broadcast_multiply_fusion = f32[32,4096]{1,0:T(8,128)} fusion(f32[32,4096]{1,0:T(8,128)} %reduce-scatter.2.cloned.1.call-done, f32[]{:T(128)S(6)} %rsqrt.3), kind=kLoop, calls=%fused_computation.1 | loop fusion | flops 131072 | bytes 1048580 | tf_op jit(solution)/shard_map/mul | solution.py:223
Async XLA Ops:
  7.2 84.3 %all-gather.3.cloned.1.call-start = ((), (), s32[]{:S(2)}) async-start(), calls=%async_computation.4 | async-start | bytes 17301504 | tf_op jit(solution)/shard_map/all_gather | solution.py:214
  7.9 130.5 %reduce-scatter.2.cloned.1.call-start = ((), (), s32[]{:S(2)}) async-start(), calls=%async_computation.3 | async-start | bytes 2621440 | tf_op jit(solution)/shard_map/reduce_scatter | solution.py:219
  10.0 81.5 %copy-start.1 = (f32[1,32,16384]{2,1,0:T(8,128)S(1)}, f32[1,32,16384]{2,1,0:T(8,128)}, u32[]{:S(2)}) copy-start(f32[1,32,16384]{2,1,0:T(8,128)} %param.3) | copy-start | bytes 6291460
  10.0 81.5 %copy-start.3 = (s32[64]{0:T(128)S(1)}, s32[64]{0:T(128)}, u32[]{:S(2)}) copy-start(s32[64]{0:T(128)} %reshape.7.pos_ref) | copy-start | bytes 772
  10.0 81.5 %copy-start.4 = (s32[2]{0:T(128)S(1)}, s32[2]{0:T(128)}, u32[]{:S(2)}) copy-start(s32[2]{0:T(128)} %pad_add_fusion.id_ref) | copy-start | bytes 28
  91.5 5.8 %copy-start = (f32[1,2048,2048]{2,1,0:T(8,128)S(1)}, f32[1,2048,2048]{2,1,0:T(8,128)}, u32[]{:S(2)}) copy-start(f32[1,2048,2048]{2,1,0:T(8,128)} %all-gather.3.cloned.1.call-done) | copy-start | bytes 50331652
  97.3 0.9 copy-start.2
Sparse Core Ops, SparseCore 0:
  10.2 81.2 all-gather.2
  109.7 28.5 reduce-scatter.1

commit v2 on v1

--- a/solution.py
+++ b/solution.py
@@ -22,6 +22,16 @@
 NCOL = 16384
 TALL = SLAB + SUBLANES
 FOLD = LANES // STEPS
+QUARTER = NCOL // NCHAN
+PIECES = (
+    (0, 0, 32),
+    (1, 0, 16),
+    (1, 16, 16),
+    (2, 0, 16),
+    (2, 16, 16),
+    (3, 0, 16),
+    (3, 16, 16),
+)
 
 
 def floor_to(x, size):
@@ -130,7 +140,8 @@
     )(ids, parts)
 
 
-def apply_kernel(pos_ref, id_ref, amps_ref, psf_ref, res_ref, out_ref, image, windows, sems, edge_sems):
+def apply_kernel(pos_ref, id_ref, amps_ref, psf_ref, res_ref, out_ref, *rest):
+    *piece_refs, image, windows, sems, edge_sems = rest
     first = id_ref[0] * SLAB
     lane = lax.broadcasted_iota(jnp.int32, (SUBLANES, LANES), 1)
     sub = lax.broadcasted_iota(jnp.int32, (SUBLANES, LANES), 0)
@@ -176,32 +187,54 @@
         return 0
 
     lax.fori_loop(0, STEPS, peak, 0)
-    store = pltpu.make_async_copy(image.at[:, pl.ds(0, NCOL)], out_ref, edge_sems.at[1])
-    store.start()
-    store.wait()
+    copies = [pltpu.make_async_copy(image.at[:, pl.ds(0, NCOL)], out_ref, edge_sems.at[0])]
+    for n, ((ahead, top, tall), piece) in enumerate(zip(PIECES, piece_refs)):
+        col = pl.multiple_of(((id_ref[1] + ahead) & (NCHAN - 1)) * QUARTER, QUARTER)
+        src = image.at[pl.ds(top, tall), pl.ds(col, QUARTER)]
+        copies.append(pltpu.make_async_copy(src, piece, edge_sems.at[n + 1]))
+    for copy in reversed(copies):
+        copy.start()
+    for copy in copies:
+        copy.wait()
 
 
 def apply(pos, ids, amps, psf, residual):
+    hbm = pl.BlockSpec(memory_space=pltpu.HBM)
     return pl.pallas_call(
         apply_kernel,
-        out_shape=jax.ShapeDtypeStruct((SLAB, NCOL), jnp.float32),
+        out_shape=[
+            jax.ShapeDtypeStruct((SLAB, NCOL), jnp.float32),
+            *(jax.ShapeDtypeStruct((tall, QUARTER), jnp.float32) for _, _, tall in PIECES),
+        ],
         in_specs=[
             pl.BlockSpec(memory_space=pltpu.SMEM),
             pl.BlockSpec(memory_space=pltpu.SMEM),
             pl.BlockSpec(memory_space=pltpu.VMEM),
-            pl.BlockSpec(memory_space=pl.ANY),
-            pl.BlockSpec(memory_space=pl.ANY),
-        ],
-        out_specs=pl.BlockSpec(memory_space=pl.ANY),
+            hbm,
+            hbm,
+        ],
+        out_specs=[hbm] + [pl.BlockSpec(memory_space=pl.ANY)] * len(PIECES),
         scratch_shapes=[
             pltpu.VMEM((SLAB, NCOL + LANES), jnp.float32),
             pltpu.VMEM((STEPS, TALL, PATCH), jnp.float32),
             pltpu.SemaphoreType.DMA((STEPS,)),
-            pltpu.SemaphoreType.DMA((2,)),
-        ],
-        compiler_params=pltpu.CompilerParams(vmem_limit_bytes=32 << 20),
+            pltpu.SemaphoreType.DMA((len(PIECES) + 1,)),
+        ],
+        compiler_params=pltpu.CompilerParams(vmem_limit_bytes=52 << 20),
         name="apply",
     )(pos, ids, amps, psf, residual)
+
+
+def channel_sum(pieces):
+    mine, right_top, right_low, far_top, far_low, left_top, left_low = pieces
+
+    def shift(x, by):
+        return lax.ppermute(x, "chan", [(i, (i + by) % NCHAN) for i in range(NCHAN)])
+
+    far_top, far_low = shift(far_top, 1), shift(far_low, 3)
+    from_left_low, from_right_top = shift(right_low, 1), shift(left_top, 3)
+    from_left_top, from_right_low = shift(right_top + far_top, 1), shift(left_low + far_low, 3)
+    return mine + jnp.concatenate([from_left_top + from_right_top, from_left_low + from_right_low], 0)
 
 
 def on_device(residual, psf, positions):
@@ -215,8 +248,8 @@
     parts = table(pos, ids, psf[0], residual[0])
     parts = lax.all_to_all(parts, CHAN_ROWS, 0, 0, tiled=True)
     amps = solve(ids, parts)
-    image = apply(pos, ids, amps, full_psf, residual[0])
-    summed = lax.psum_scatter(image, "chan", scatter_dimension=1, tiled=True)
+    image, *pieces = apply(pos, ids, amps, full_psf, residual[0])
+    summed = channel_sum(pieces)
     square = jnp.broadcast_to(jnp.sum(summed * summed), (DEVICES, 1, LANES))
     total = jnp.sum(lax.all_to_all(square, CHAN_ROWS, 0, 0, tiled=True)[:, 0, 0])
     count = slab * nrows * ncols

time: 169 us -> 150 us (0.89)
  waiting for transfers between devices: 70 us -> 54.5 us
  starting transfers between devices: 0.08 us -> 7.04 us
  local copies, waits for them, and re-layouts: 8.74 us -> 2.98 us
  Pallas kernels: 27.2 us -> 25.2 us
  other arithmetic: 5.03 us -> 3.05 us
    reduce_scatter x1 -> x0, waiting for transfers between devices: 28.8 us -> none  [on_device(): summed = lax.psum_scatter(image, 'chan', scatter_dimension=1, tiled=True)]
    ppermute x0 -> x6, waiting for transfers between devices: none -> 13 us  [shift(): lax.ppermute(x, 'chan', [(i, (i + by) % NCHAN) for i in range(NCHAN)])]
    ppermute x0 -> x6, starting transfers between devices: none -> 7.01 us  [shift(): lax.ppermute(x, 'chan', [(i, (i + by) % NCHAN) for i in range(NCHAN)])]
    unnamed x11 -> x9, local copies, waits for them, and re-layouts: 7.44 us -> 1.68 us
    pallas_call x1, Pallas kernels: 11.4 us -> 9.54 us  [apply(): pl.pallas_call(apply_kernel, out_shape=[jax.ShapeDtypeStruct((SLAB, NCOL)...]
  transfers between devices with their start and end apart: 2 -> 7, of which waited for: 2 -> 4; matrix products, arithmetic and copies ran while one was open for 1% -> 1% of each run, Pallas kernels for 9% -> 10%
where the time goes in v2:
time: 150 us
  waiting for transfers between devices  54.5 us (36%)
  blocking collectives  42.5 us (28%)
  Pallas kernels  25.2 us (17%)
  between operations  14.8 us (10%)
  starting transfers between devices  7.04 us (5%)
  other arithmetic  3.05 us (2%)
  local copies, waits for them, and re-layouts  2.98 us (2%)
    all_gather x1, waiting for transfers between devices, on_device(): full_psf = lax.all_gather(psf[0], ROWS, axis=0, tiled=True)  40.8 us
    all_to_all x1, blocking collectives, on_device(): parts = lax.all_to_all(parts, CHAN_ROWS, 0, 0, tiled=True)  25.1 us
    all_to_all x1, blocking collectives, on_device(): lax.all_to_all(square, CHAN_ROWS, 0, 0, tiled=True)[:, 0, 0]  17.4 us
    ppermute x6, waiting for transfers between devices, shift(): lax.ppermute(x, 'chan', [(i, (i + by) % NCHAN) for i in range(NCHAN)])  13 us
    pallas_call x1, Pallas kernels, table(): pl.pallas_call(table_kernel, out_shape=jax.ShapeDtypeStruct((DEVICES, SUB...  11.1 us
    pallas_call x1, Pallas kernels, apply(): pl.pallas_call(apply_kernel, out_shape=[jax.ShapeDtypeStruct((SLAB, NCOL)...  9.54 us
    ppermute x6, starting transfers between devices, shift(): lax.ppermute(x, 'chan', [(i, (i + by) % NCHAN) for i in range(NCHAN)])  7.01 us
    pallas_call x1, Pallas kernels, solve(): pl.pallas_call(solve_kernel, out_shape=jax.ShapeDtypeStruct((STEPS, SUBLA...  4.59 us
  transfers between devices with their start and end apart: 7, of which 4 were waited for; matrix products, arithmetic and copies ran while one was open for 1% of the time, Pallas kernels for 10%

profile of v2, /device:TPU:1, one launch (start us, length us, event | category | flops | bytes accessed | tf_op | source)
XLA Modules:
  0.0 150.1 jit_solution(457499387580389570)
XLA Ops:
  7.2 0.0 all-gather.3.cloned.1.call-start
  7.2 0.7 all-gather.3.cloned.1.call-update
  7.9 0.8 copy.8
  8.7 0.6 reshape.7.pos_ref
  9.3 0.6 pad_add_fusion.id_ref
  9.9 0.0 copy-start.1
  9.9 0.0 copy-start.2
  9.9 11.1 %table.1 = f32[128,8,128]{2,1,0:T(8,128)} custom-call(s32[64]{0:T(128)} %reshape.7.pos_ref, s32[2]{0:T(128)} %pad_add_fusion.id_ref, f32[64,2048]{1,0:T(8,128)} %bitcast.9, f32[32,16384]{1,0:T(8,128)} %bitcast.7), custom_call_target="tpu_custom_call" | custom-call | tf_op jit(solution)/shard_map/table/pallas_call | solution.py:85
  21.0 25.1 %all_to_all.10.parts_ref = f32[128,8,128]{2,1,0:T(8,128)} all-to-all(f32[128,8,128]{2,1,0:T(8,128)} %table.1), channel_id=1, replica_groups=mesh['chan'=4,'rows_0'=4,'rows_1'=4,'rows_2'=2] {'chan','rows_0','rows_1..., dimensions={0} | all-to-all | bytes 1048576 | tf_op jit(solution)/shard_map/all_to_all | solution.py:249
  46.1 4.6 %solve.1.amps_ref = f32[32,8,128]{2,1,0:T(8,128)} custom-call(s32[2]{0:T(128)} %pad_add_fusion.id_ref, f32[128,8,128]{2,1,0:T(8,128)} %all_to_all.10.parts_ref), custom_call_target="tpu_custom_call" | custom-call | tf_op jit(solution)/shard_map/solve/pallas_call | solution.py:133
  50.7 40.8 %all-gather.3.cloned.1.call-done = f32[1,2048,2048]{2,1,0:T(8,128)} async-done(((f32[1,64,2048]{2,1,0:T(8,128)}), f32[1,2048,2048]{2,1,0:T(8,128)}) %all-gather.3.cloned.1.call-update) | async-done | bytes 16777232 | tf_op jit(solution)/shard_map/all_gather | solution.py:247
  91.5 0.0 copy-done.1
  91.5 0.0 copy-done.2
  91.5 0.0 copy-start
  91.5 0.9 copy-done
  92.4 9.5 %apply.1 = (f32[32,16384]{1,0:T(8,128)}, f32[32,4096]{1,0:T(8,128)}, f32[16,4096]{1,0:T(8,128)S(1)}, f32[16,4096]{1,0:T(8,128)S(1)}, f32[16,4096]{1,0:T(8,128)S(...) custom-call(s32[64]{0:T(128)S(1)} %copy-done.1, s32[2]{0:T(128)S(1)} %copy-done.2, ...), custom_call_target="tpu_custom_call" | custom-call | tf_op jit(solution)/shard_map/apply/pallas_call | solution.py:203
  102.0 0.0 copy-start.3
  102.0 1.3 collective-permute-start
  103.3 1.5 collective-permute-start.4
  104.7 1.2 collective-permute-start.2
  105.9 0.3 collective-permute-start.3
  106.2 4.7 %collective-permute-done = f32[16,4096]{1,0:T(8,128)S(1)} collective-permute-done((f32[16,4096]{1,0:T(8,128)S(1)}, f32[16,4096]{1,0:T(8,128)S(1)}, u32[]{:S(2)}, u32[]{:S(2)}) %collective-permute-start) | collective-permute-done | bytes 262176 | tf_op jit(solution)/shard_map/ppermute | solution.py:232
  110.9 0.1 collective-permute-start.1
  111.0 0.0 collective-permute-done.4
  111.0 2.7 %collective-permute-start.5 = (f32[16,4096]{1,0:T(8,128)S(1)}, f32[16,4096]{1,0:T(8,128)S(1)}, u32[]{:S(2)}, u32[]{:S(2)}) collective-permute-start(f32[16,4096]{1,0:T(8,128)S(1)} %add.28), channel_id=1, source_target_pairs={{0,96},{32,0},{64,32},{96,64},{1,97},{33,1},{65,33},{97,65},{2,98}... | collective-permute-start | bytes 786440 | tf_op jit(solution)/shard_map/ppermute | solution.py:232
  113.8 2.4 %collective-permute-done.2 = f32[16,4096]{1,0:T(8,128)S(1)} collective-permute-done((f32[16,4096]{1,0:T(8,128)S(1)}, f32[16,4096]{1,0:T(8,128)S(1)}, u32[]{:S(2)}, u32[]{:S(2)}) %collective-permute-start.2) | collective-permute-done | bytes 262176 | tf_op jit(solution)/shard_map/ppermute | solution.py:232
  116.2 5.9 %collective-permute-done.1 = f32[16,4096]{1,0:T(8,128)S(1)} collective-permute-done((f32[16,4096]{1,0:T(8,128)S(1)}, f32[16,4096]{1,0:T(8,128)S(1)}, u32[]{:S(2)}, u32[]{:S(2)}) %collective-permute-start.1) | collective-permute-done | bytes 262176 | tf_op jit(solution)/shard_map/ppermute | solution.py:232
  122.1 0.0 collective-permute-done.3
  122.2 0.0 collective-permute-done.5
  122.2 0.0 copy-done.3
  122.2 0.7 multiply_reduce_fusion
  123.0 0.7 broadcast_in_dim.7
  123.6 17.4 %all_to_all.11 = f32[128,1,128]{2,1,0:T(1,128)S(1)} all-to-all(f32[128,1,128]{2,1,0:T(1,128)S(1)} %broadcast_in_dim.7), channel_id=1, replica_groups=mesh['chan'=4,'rows_0'=4,'rows_1'=4,'rows_2'=2] {'chan','rows_0','rows_1..., dimensions={0} | all-to-all | bytes 131072 | tf_op jit(solution)/shard_map/all_to_all | solution.py:254
  141.0 0.7 slice_reduce_fusion
  142.5 0.8 broadcast_multiply_fusion
  (4 shorter events, 0.1 us)
Async XLA Ops:
  7.2 84.4 %all-gather.3.cloned.1.call-start = ((), (), s32[]{:S(2)}) async-start(), calls=%async_computation.2 | async-start | bytes 17301504 | tf_op jit(solution)/shard_map/all_gather | solution.py:247
  9.9 81.6 %copy-start.1 = (s32[64]{0:T(128)S(1)}, s32[64]{0:T(128)}, u32[]{:S(2)}) copy-start(s32[64]{0:T(128)} %reshape.7.pos_ref) | copy-start | bytes 772
  9.9 81.6 %copy-start.2 = (s32[2]{0:T(128)S(1)}, s32[2]{0:T(128)}, u32[]{:S(2)}) copy-start(s32[2]{0:T(128)} %pad_add_fusion.id_ref) | copy-start | bytes 28
  91.5 0.9 copy-start
  102.0 20.2 %copy-start.3 = (f32[32,4096]{1,0:T(8,128)S(1)}, f32[32,4096]{1,0:T(8,128)}, u32[]{:S(2)}) copy-start(f32[32,4096]{1,0:T(8,128)} %get-tuple-element.11) | copy-start | bytes 1572868
  102.0 8.9 %collective-permute-start = (f32[16,4096]{1,0:T(8,128)S(1)}, f32[16,4096]{1,0:T(8,128)S(1)}, u32[]{:S(2)}, u32[]{:S(2)}) collective-permute-start(f32[16,4096]{1,0:T(8,128)S(1)} %get-tuple-element.13), channel_id=1, source_target_pairs={{0,32},{32,64},{64,96},{96,0},{1,33},{33,65},{65,97},{97,1},{2,34}... | collective-permute-start | bytes 786440 | tf_op jit(solution)/shard_map/ppermute | solution.py:232
  103.3 7.7 %collective-permute-start.4 = (f32[16,4096]{1,0:T(8,128)S(1)}, f32[16,4096]{1,0:T(8,128)S(1)}, u32[]{:S(2)}, u32[]{:S(2)}) collective-permute-start(f32[16,4096]{1,0:T(8,128)S(1)} %get-tuple-element.17), channel_id=1, source_target_pairs={{0,96},{32,0},{64,32},{96,64},{1,97},{33,1},{65,33},{97,65},{2,98}... | collective-permute-start | bytes 786440 | tf_op jit(solution)/shard_map/ppermute | solution.py:232
  104.7 11.5 %collective-permute-start.2 = (f32[16,4096]{1,0:T(8,128)S(1)}, f32[16,4096]{1,0:T(8,128)S(1)}, u32[]{:S(2)}, u32[]{:S(2)}) collective-permute-start(f32[16,4096]{1,0:T(8,128)S(1)} %get-tuple-element.14), channel_id=1, source_target_pairs={{0,96},{32,0},{64,32},{96,64},{1,97},{33,1},{65,33},{97,65},{2,98}... | collective-permute-start | bytes 786440 | tf_op jit(solution)/shard_map/ppermute | solution.py:232
  105.9 16.2 %collective-permute-start.3 = (f32[16,4096]{1,0:T(8,128)S(1)}, f32[16,4096]{1,0:T(8,128)S(1)}, u32[]{:S(2)}, u32[]{:S(2)}) collective-permute-start(f32[16,4096]{1,0:T(8,128)S(1)} %get-tuple-element.15), channel_id=1, source_target_pairs={{0,32},{32,64},{64,96},{96,0},{1,33},{33,65},{65,97},{97,1},{2,34}... | collective-permute-start | bytes 786440 | tf_op jit(solution)/shard_map/ppermute | solution.py:232
  110.9 11.2 %collective-permute-start.1 = (f32[16,4096]{1,0:T(8,128)S(1)}, f32[16,4096]{1,0:T(8,128)S(1)}, u32[]{:S(2)}, u32[]{:S(2)}) collective-permute-start(f32[16,4096]{1,0:T(8,128)S(1)} %add.26), channel_id=1, source_target_pairs={{0,32},{32,64},{64,96},{96,0},{1,33},{33,65},{65,97},{97,1},{2,34}... | collective-permute-start | bytes 786440 | tf_op jit(solution)/shard_map/ppermute | solution.py:232
  111.0 11.1 %collective-permute-start.5 = (f32[16,4096]{1,0:T(8,128)S(1)}, f32[16,4096]{1,0:T(8,128)S(1)}, u32[]{:S(2)}, u32[]{:S(2)}) collective-permute-start(f32[16,4096]{1,0:T(8,128)S(1)} %add.28), channel_id=1, source_target_pairs={{0,96},{32,0},{64,32},{96,64},{1,97},{33,1},{65,33},{97,65},{2,98}... | collective-permute-start | bytes 786440 | tf_op jit(solution)/shard_map/ppermute | solution.py:232
Sparse Core Ops, SparseCore 0:
  10.2 81.2 all-gather.2
